TPU v7x, 32 devices: a whole 2x2x4 slice. The times are simulated.
32 devices in a mesh: tok: 8 (over z, y), vocab: 4 (over x, core).
Axes of the slice: x: 2, y: 2, z: 4, core: 2. Of those that a mesh axis runs over, the one named last changes fastest.
Arguments:
- hidden: bfloat16 [192, 9216], P('tok'), may hold values from -256 to 256
- policy_head: bfloat16 [9216, 32768], P(None, ('tok', 'vocab')), may hold values from -0.0625 to 0.0625
- reference_head: bfloat16 [9216, 32768], P(None, ('tok', 'vocab')), may hold values from -0.0625 to 0.0625
- targets: int32 [192], P('tok'), may hold values from 0 to 32767
Outputs:
- policy_logprob: float32 [192], P('tok')
- reference_logprob: float32 [192], P('tok')
- divergence: float32 [192], P('tok')
All inputs are finite; a program needn't handle non-finite values.
Results may differ from a plain program's by a relative error of at most 0.00055.
Values may be sent and summed in bfloat16 or wider, within the bound.
A program may use at most 128 MiB of HBM per device.

v0:
```python
import jax
import jax.numpy as jnp
from jax import lax
from jax.sharding import PartitionSpec as P


def combined_all(value, axis, combine):
    everything = jax.tree.map(lambda part: lax.all_gather(part, axis), value)
    leading = jax.tree.map(lambda part: part[0], everything)

    def step(k, so_far):
        return combine(so_far, jax.tree.map(lambda part: part[k], everything))

    return lax.fori_loop(1, lax.axis_size(axis), step, leading)


def local_sums(policy_logits, reference_logits, target_hits, peak_policy, peak_reference):
    policy_exp = jnp.exp(policy_logits - peak_policy[:, None])
    reference_exp = jnp.exp(reference_logits - peak_reference[:, None])
    total_policy = jnp.sum(policy_exp, axis=1)
    total_reference = jnp.sum(reference_exp, axis=1)
    weighted = jnp.sum(policy_exp * (policy_logits - reference_logits), axis=1)
    target_policy = jnp.sum(jnp.where(target_hits, policy_logits, 0.0), axis=1)
    target_reference = jnp.sum(jnp.where(target_hits, reference_logits, 0.0), axis=1)
    return (total_policy, total_reference, weighted, target_policy, target_reference)


def local_stats(policy_logits, reference_logits, target_hits):
    peak_policy = jnp.max(policy_logits, axis=1)
    peak_reference = jnp.max(reference_logits, axis=1)
    summed = local_sums(policy_logits, reference_logits, target_hits, peak_policy, peak_reference)
    return (peak_policy, peak_reference) + summed


def combine_stats(left_stats, right_stats):
    peak_policy = jnp.maximum(left_stats[0], right_stats[0])
    peak_reference = jnp.maximum(left_stats[1], right_stats[1])
    left_policy = jnp.exp(left_stats[0] - peak_policy)
    right_policy = jnp.exp(right_stats[0] - peak_policy)
    left_reference = jnp.exp(left_stats[1] - peak_reference)
    right_reference = jnp.exp(right_stats[1] - peak_reference)
    return (
        peak_policy,
        peak_reference,
        left_stats[2] * left_policy + right_stats[2] * right_policy,
        left_stats[3] * left_reference + right_stats[3] * right_reference,
        left_stats[4] * left_policy + right_stats[4] * right_policy,
        left_stats[5] + right_stats[5],
        left_stats[6] + right_stats[6],
    )


def combine_senders(received):
    peak_policy = jnp.max(received[0], axis=0)
    peak_reference = jnp.max(received[1], axis=0)
    policy_scale = jnp.exp(received[0] - peak_policy[None, :])
    reference_scale = jnp.exp(received[1] - peak_reference[None, :])
    return (
        peak_policy,
        peak_reference,
        jnp.sum(received[2] * policy_scale, axis=0),
        jnp.sum(received[3] * reference_scale, axis=0),
        jnp.sum(received[4] * policy_scale, axis=0),
        jnp.sum(received[5], axis=0),
        jnp.sum(received[6], axis=0),
    )


def finish(merged_stats):
    log_norm_policy = merged_stats[0] + jnp.log(merged_stats[2])
    log_norm_reference = merged_stats[1] + jnp.log(merged_stats[3])
    policy_logprob = merged_stats[5] - log_norm_policy
    reference_logprob = merged_stats[6] - log_norm_reference
    divergence = merged_stats[4] / merged_stats[2] - log_norm_policy + log_norm_reference
    return (policy_logprob, reference_logprob, divergence)


def body(hidden, policy_head, reference_head, targets):
    tok_count = lax.axis_size("tok")
    vocab_count = lax.axis_size("vocab")
    tok_rows = hidden.shape[0]
    vocab_cols = policy_head.shape[1]
    piece = lax.all_gather(hidden, "tok", axis=0, tiled=True)
    summed = jnp.concatenate(
        [
            jnp.dot(piece, policy_head, preferred_element_type=jnp.float32),
            jnp.dot(piece, reference_head, preferred_element_type=jnp.float32),
        ],
        axis=1,
    )
    policy_logits = summed[:, :vocab_cols]
    reference_logits = summed[:, vocab_cols:]
    every_target = lax.all_gather(targets, "tok", axis=0, tiled=True)
    block_index = lax.axis_index("tok") * vocab_count + lax.axis_index("vocab")
    vocab_ids = block_index * vocab_cols + lax.iota(jnp.int32, vocab_cols)
    target_hits = vocab_ids[None, :] == every_target[:, None]
    partial_value = local_stats(policy_logits, reference_logits, target_hits)
    shaped = tuple((entry.reshape(tok_count, tok_rows) for entry in partial_value))
    received = lax.all_to_all(shaped, "tok", split_axis=0, concat_axis=0, tiled=True)
    own_stats = combine_senders(received)
    merged_stats = combined_all(own_stats, "vocab", combine_stats)
    return finish(merged_stats)


def solution(mesh):
    in_specs = (P("tok", None), P(None, ("tok", "vocab")), P(None, ("tok", "vocab")), P("tok"))
    out_specs = (P("tok"), P("tok"), P("tok"))
    return jax.shard_map(body, mesh=mesh, in_specs=in_specs, out_specs=out_specs, check_vma=False)
```

profile of v0, /device:TPU:0, one launch (start us, length us, event | category | flops | bytes accessed | tf_op | source)
XLA Modules:
  0.0 179.8 jit_solution(15287167651976823062)
XLA Ops:
  7.2 0.7 all-gather.9.cloned.1.call-update
  7.9 1.2 dynamic-slice.5
  9.8 0.9 dynamic-update-slice.5
  10.7 13.1 %all-reduce.5 = s32[192]{0:T(256)S(1)} all-reduce(s32[192]{0:T(256)S(1)} %dynamic-update-slice.5), channel_id=1, replica_groups=mesh['tok'=8,'vocab'=4] {'tok'}, use_global_device_ids=true, to_apply=%add.5 | all-reduce | flops 192 | bytes 1536
  23.8 53.8 %all-gather.9.cloned.1.call-done = bf16[192,9216]{1,0:T(8,128)(2,1)} async-done(((bf16[24,9216]{1,0:T(8,128)(2,1)}), bf16[192,9216]{1,0:T(8,128)(2,1)}) %all-gather.9.cloned.1.call-update) | async-done | bytes 3538960 | tf_op jit(solution)/shard_map/all_gather | solution.py:83
  77.5 9.6 %fusion.24 = (f32[192]{0:T(256)S(1)}, f32[192,1024]{1,0:T(8,128)S(1)}) fusion(bf16[192,9216]{1,0:T(8,128)(2,1)} %all-gather.9.cloned.1.call-done, bf16[9216,1024]{1,0:T(8,128)(2,1)} %param.7), kind=kOutput, calls=%fused_computation.44 | convolution fusion | flops 3624075008 | bytes 23200512 | tf_op jit(solution)/shard_map/dot_general | solution.py:86
  87.2 3.1 %copy-done = bf16[9216,1024]{1,0:T(8,128)(2,1)S(1)} copy-done((bf16[9216,1024]{1,0:T(8,128)(2,1)S(1)}, bf16[9216,1024]{1,0:T(8,128)(2,1)}, u32[]{:S(2)}) %copy-start) | copy-done | bytes 18874392
  90.3 5.9 %fusion.25 = (f32[192]{0:T(256)S(1)}, f32[192,1024]{1,0:T(8,128)S(1)}) fusion(bf16[192,9216]{1,0:T(8,128)(2,1)} %all-gather.9.cloned.1.call-done, bf16[9216,1024]{1,0:T(8,128)(2,1)S(1)} %copy-done), kind=kOutput, calls=%fused_computation.45 | convolution fusion | flops 3624075008 | bytes 23200512 | tf_op jit(solution)/shard_map/dot_general | solution.py:87
  96.2 0.7 multiply_reduce_fusion
  96.9 0.7 all_to_all.64
  97.5 3.3 %all-to-all-start.4 = ((f32[8,1,24]{2,1,0:T(1,128)}), f32[8,1,24]{2,1,0:T(1,128)S(1)}, u32[]{:S(2)}, u32[]{:S(2)}) async-start(f32[8,1,24]{2,1,0:T(1,128)} %all_to_all.64), calls=%async_computation.4 | async-start | bytes 8192 | tf_op jit(solution)/shard_map/all_to_all | solution.py:99
  100.9 0.7 all_to_all.56
  101.6 5.8 %all-to-all-done.4 = f32[8,1,24]{2,1,0:T(1,128)S(1)} async-done(((f32[8,1,24]{2,1,0:T(1,128)}), f32[8,1,24]{2,1,0:T(1,128)S(1)}, u32[]{:S(2)}, u32[]{:S(2)}) %all-to-all-start.4) | async-done | bytes 800 | tf_op jit(solution)/shard_map/all_to_all | solution.py:99
  107.4 3.2 %all-to-all-start.2 = ((f32[8,1,24]{2,1,0:T(1,128)}), f32[8,1,24]{2,1,0:T(1,128)S(1)}, u32[]{:S(2)}, u32[]{:S(2)}) async-start(f32[8,1,24]{2,1,0:T(1,128)} %all_to_all.56), calls=%async_computation.2 | async-start | bytes 8192 | tf_op jit(solution)/shard_map/all_to_all | solution.py:99
  110.6 0.7 all_to_all.52
  111.3 5.7 %all-to-all-done.2 = f32[8,1,24]{2,1,0:T(1,128)S(1)} async-done(((f32[8,1,24]{2,1,0:T(1,128)}), f32[8,1,24]{2,1,0:T(1,128)S(1)}, u32[]{:S(2)}, u32[]{:S(2)}) %all-to-all-start.2) | async-done | bytes 800 | tf_op jit(solution)/shard_map/all_to_all | solution.py:99
  117.1 3.3 %all-to-all-start = ((f32[8,1,24]{2,1,0:T(1,128)}), f32[8,1,24]{2,1,0:T(1,128)S(1)}, u32[]{:S(2)}, u32[]{:S(2)}) async-start(f32[8,1,24]{2,1,0:T(1,128)} %all_to_all.52), calls=%async_computation | async-start | bytes 8192 | tf_op jit(solution)/shard_map/all_to_all | solution.py:99
  120.4 0.7 all_to_all.60
  121.1 5.8 %all-to-all-done = f32[8,1,24]{2,1,0:T(1,128)S(1)} async-done(((f32[8,1,24]{2,1,0:T(1,128)}), f32[8,1,24]{2,1,0:T(1,128)S(1)}, u32[]{:S(2)}, u32[]{:S(2)}) %all-to-all-start) | async-done | bytes 800 | tf_op jit(solution)/shard_map/all_to_all | solution.py:99
  126.8 3.2 %all-to-all-start.3 = ((f32[8,1,24]{2,1,0:T(1,128)}), f32[8,1,24]{2,1,0:T(1,128)S(1)}, u32[]{:S(2)}, u32[]{:S(2)}) async-start(f32[8,1,24]{2,1,0:T(1,128)} %all_to_all.60), calls=%async_computation.3 | async-start | bytes 8192 | tf_op jit(solution)/shard_map/all_to_all | solution.py:99
  130.1 0.7 all_to_all.54
  130.8 5.7 %all-to-all-done.3 = f32[8,1,24]{2,1,0:T(1,128)S(1)} async-done(((f32[8,1,24]{2,1,0:T(1,128)}), f32[8,1,24]{2,1,0:T(1,128)S(1)}, u32[]{:S(2)}, u32[]{:S(2)}) %all-to-all-start.3) | async-done | bytes 800 | tf_op jit(solution)/shard_map/all_to_all | solution.py:99
  136.5 3.3 %all-to-all-start.1 = ((f32[8,1,24]{2,1,0:T(1,128)}), f32[8,1,24]{2,1,0:T(1,128)S(1)}, u32[]{:S(2)}, u32[]{:S(2)}) async-start(f32[8,1,24]{2,1,0:T(1,128)} %all_to_all.54), calls=%async_computation.1 | async-start | bytes 8192 | tf_op jit(solution)/shard_map/all_to_all | solution.py:99
  139.9 0.6 dynamic-slice
  141.1 0.7 all_to_all.67
  141.8 0.7 all_to_all.69
  142.5 3.8 %all-to-all-done.1 = f32[8,1,24]{2,1,0:T(1,128)S(1)} async-done(((f32[8,1,24]{2,1,0:T(1,128)}), f32[8,1,24]{2,1,0:T(1,128)S(1)}, u32[]{:S(2)}, u32[]{:S(2)}) %all-to-all-start.1) | async-done | bytes 800 | tf_op jit(solution)/shard_map/all_to_all | solution.py:99
  146.3 3.2 %all-to-all-start.5 = ((f32[8,1,24]{2,1,0:T(1,128)}), f32[8,1,24]{2,1,0:T(1,128)S(1)}, u32[]{:S(2)}, u32[]{:S(2)}) async-start(f32[8,1,24]{2,1,0:T(1,128)} %all_to_all.67), calls=%async_computation.5 | async-start | bytes 8192 | tf_op jit(solution)/shard_map/all_to_all | solution.py:99
  149.6 6.4 %all-to-all-done.5 = f32[8,1,24]{2,1,0:T(1,128)S(1)} async-done(((f32[8,1,24]{2,1,0:T(1,128)}), f32[8,1,24]{2,1,0:T(1,128)S(1)}, u32[]{:S(2)}, u32[]{:S(2)}) %all-to-all-start.5) | async-done | bytes 800 | tf_op jit(solution)/shard_map/all_to_all | solution.py:99
  156.0 3.3 %all-to-all-start.6 = ((f32[8,1,24]{2,1,0:T(1,128)}), f32[8,1,24]{2,1,0:T(1,128)S(1)}, u32[]{:S(2)}, u32[]{:S(2)}) async-start(f32[8,1,24]{2,1,0:T(1,128)} %all_to_all.69), calls=%async_computation.6 | async-start | bytes 8192 | tf_op jit(solution)/shard_map/all_to_all | solution.py:99
  159.3 0.2 dynamic-update-slice
  159.5 0.2 dynamic-update-slice.1
  159.7 0.2 dynamic-update-slice.4
  159.9 0.2 dynamic-update-slice.2
  160.1 0.2 dynamic-update-slice.3
  160.4 0.2 dynamic-update-slice.6
  160.6 5.1 %all-to-all-done.6 = f32[8,1,24]{2,1,0:T(1,128)S(1)} async-done(((f32[8,1,24]{2,1,0:T(1,128)}), f32[8,1,24]{2,1,0:T(1,128)S(1)}, u32[]{:S(2)}, u32[]{:S(2)}) %all-to-all-start.6) | async-done | bytes 800 | tf_op jit(solution)/shard_map/all_to_all | solution.py:99
  165.7 0.2 dynamic-update-slice.7
  165.9 5.6 %all-reduce.8 = (f32[96]{0:T(128)S(1)}, f32[96]{0:T(128)S(1)}, f32[96]{0:T(128)S(1)}, f32[96]{0:T(128)S(1)}, f32[96]{0:T(128)S(1)}, /*index=5*/f32[96]{0:T(128)S(1)}, f32[96]{0:T(128)S(1)}) all-reduce(f32[96]{0:T(128)S(1)} %dynamic-update-slice, f32[96]{0:T(128)S(1)} %dynamic-update-slice.1, ...), channel_id=2, replica_groups=mesh['tok'=8,'vocab'=4] {'vocab'}, use_global_device_ids=true, to_apply=%add | all-reduce | flops 672 | bytes 5376
  171.6 0.1 reshape.43
  171.7 0.1 reshape.44
  171.7 0.1 reshape.45
  171.8 0.1 reshape.46
  171.9 0.1 reshape.47
  172.0 0.1 reshape.48
  172.1 0.1 reshape.49
  172.2 0.3 while.27
  172.5 0.5 subtract_add_fusion
  (31 shorter events, 0.4 us)
Async XLA Ops:
  7.2 70.3 %all-gather.9.cloned.1.call-start = ((), (), s32[]{:S(2)}) async-start(), calls=%async_computation.7 | async-start | bytes 3981312 | tf_op jit(solution)/shard_map/all_gather | solution.py:83
  77.5 12.7 %copy-start = (bf16[9216,1024]{1,0:T(8,128)(2,1)S(1)}, bf16[9216,1024]{1,0:T(8,128)(2,1)}, u32[]{:S(2)}) copy-start(bf16[9216,1024]{1,0:T(8,128)(2,1)} %param.8) | copy-start | bytes 56623108
  90.3 49.6 %copy-start.1 = (u32[32]{0:T(128)S(1)}, u32[32]{0:T(128)}, u32[]{:S(2)}) copy-start(u32[32]{0:T(128)} %constant.57) | copy-start | bytes 388
  97.5 9.8 %all-to-all-start.4 = ((f32[8,1,24]{2,1,0:T(1,128)}), f32[8,1,24]{2,1,0:T(1,128)S(1)}, u32[]{:S(2)}, u32[]{:S(2)}) async-start(f32[8,1,24]{2,1,0:T(1,128)} %all_to_all.64), calls=%async_computation.4 | async-start | bytes 8192 | tf_op jit(solution)/shard_map/all_to_all | solution.py:99
  107.4 9.7 %all-to-all-start.2 = ((f32[8,1,24]{2,1,0:T(1,128)}), f32[8,1,24]{2,1,0:T(1,128)S(1)}, u32[]{:S(2)}, u32[]{:S(2)}) async-start(f32[8,1,24]{2,1,0:T(1,128)} %all_to_all.56), calls=%async_computation.2 | async-start | bytes 8192 | tf_op jit(solution)/shard_map/all_to_all | solution.py:99
  117.1 9.8 %all-to-all-start = ((f32[8,1,24]{2,1,0:T(1,128)}), f32[8,1,24]{2,1,0:T(1,128)S(1)}, u32[]{:S(2)}, u32[]{:S(2)}) async-start(f32[8,1,24]{2,1,0:T(1,128)} %all_to_all.52), calls=%async_computation | async-start | bytes 8192 | tf_op jit(solution)/shard_map/all_to_all | solution.py:99
  126.8 9.7 %all-to-all-start.3 = ((f32[8,1,24]{2,1,0:T(1,128)}), f32[8,1,24]{2,1,0:T(1,128)S(1)}, u32[]{:S(2)}, u32[]{:S(2)}) async-start(f32[8,1,24]{2,1,0:T(1,128)} %all_to_all.60), calls=%async_computation.3 | async-start | bytes 8192 | tf_op jit(solution)/shard_map/all_to_all | solution.py:99
  136.5 9.8 %all-to-all-start.1 = ((f32[8,1,24]{2,1,0:T(1,128)}), f32[8,1,24]{2,1,0:T(1,128)S(1)}, u32[]{:S(2)}, u32[]{:S(2)}) async-start(f32[8,1,24]{2,1,0:T(1,128)} %all_to_all.54), calls=%async_computation.1 | async-start | bytes 8192 | tf_op jit(solution)/shard_map/all_to_all | solution.py:99
  146.3 9.7 %all-to-all-start.5 = ((f32[8,1,24]{2,1,0:T(1,128)}), f32[8,1,24]{2,1,0:T(1,128)S(1)}, u32[]{:S(2)}, u32[]{:S(2)}) async-start(f32[8,1,24]{2,1,0:T(1,128)} %all_to_all.67), calls=%async_computation.5 | async-start | bytes 8192 | tf_op jit(solution)/shard_map/all_to_all | solution.py:99
  156.0 9.7 %all-to-all-start.6 = ((f32[8,1,24]{2,1,0:T(1,128)}), f32[8,1,24]{2,1,0:T(1,128)S(1)}, u32[]{:S(2)}, u32[]{:S(2)}) async-start(f32[8,1,24]{2,1,0:T(1,128)} %all_to_all.69), calls=%async_computation.6 | async-start | bytes 8192 | tf_op jit(solution)/shard_map/all_to_all | solution.py:99
Sparse Core Ops, SparseCore 0:
  10.2 67.3 all-gather.8
where the time goes:
time: 180 us
  waiting for transfers between devices  92.7 us (52%)
  starting transfers between devices  23.1 us (13%)
  blocking collectives  18.7 us (10%)
  matrix products  15.6 us (9%)
  between operations  15.5 us (9%)
  local copies, waits for them, and re-layouts  12.7 us (7%)
    all_gather x1, waiting for transfers between devices, body(): piece = lax.all_gather(hidden, 'tok', axis=0, tiled=True)  53.8 us
    all_to_all x7, waiting for transfers between devices, body(): lax.all_to_all(shaped, 'tok', split_axis=0, concat_axis=0, tiled=True)  38.3 us
    all_to_all x7, starting transfers between devices, body(): lax.all_to_all(shaped, 'tok', split_axis=0, concat_axis=0, tiled=True)  23 us
    unnamed x2, blocking collectives  18.7 us
    dot_general x1, matrix products, body(): jnp.dot(piece, policy_head, preferred_element_type=jnp.float32)  9.63 us
    unnamed x22, local copies, waits for them, and re-layouts  7.34 us
    dot_general x1, matrix products, body(): jnp.dot(piece, reference_head, preferred_element_type=jnp.float32)  5.92 us
    all_to_all x7, local copies, waits for them, and re-layouts, body(): lax.all_to_all(shaped, 'tok', split_axis=0, concat_axis=0, tiled=True)  4.75 us
  transfers between devices with their start and end apart: 8, of which 8 were waited for; matrix products, arithmetic and copies ran while one was open for 2% of the time, Pallas kernels for 0%

commit v1 on v0

--- a/solution.py
+++ b/solution.py
@@ -80,7 +80,22 @@
     vocab_count = lax.axis_size("vocab")
     tok_rows = hidden.shape[0]
     vocab_cols = policy_head.shape[1]
-    piece = lax.all_gather(hidden, "tok", axis=0, tiled=True)
+    ways, here, step_2 = (lax.axis_size("tok"), lax.axis_index("tok"), hidden.shape[0])
+    shape = [n * ways if d == 0 else n for d, n in enumerate(hidden.shape)]
+    piece = lax.dynamic_update_slice_in_dim(
+        jnp.zeros(shape, hidden.dtype), hidden, here * step_2, axis=0
+    )
+    going_up = going_down = hidden
+    for far in range(1, ways // 2 + 1):
+        going_up = lax.ppermute(going_up, "tok", [(d, (d + 1) % ways) for d in range(ways)])
+        piece = lax.dynamic_update_slice_in_dim(
+            piece, going_up, (here - far) % ways * step_2, axis=0
+        )
+        if 2 * far < ways:
+            going_down = lax.ppermute(going_down, "tok", [(d, (d - 1) % ways) for d in range(ways)])
+            piece = lax.dynamic_update_slice_in_dim(
+                piece, going_down, (here + far) % ways * step_2, axis=0
+            )
     summed = jnp.concatenate(
         [
             jnp.dot(piece, policy_head, preferred_element_type=jnp.float32),

time: 180 us -> 176 us (0.978)
  waiting for transfers between devices: 92.7 us -> 66.3 us
  starting transfers between devices: 23.1 us -> 49 us
  between operations: 15.5 us -> 2.33 us
  blocking collectives: 18.7 us -> 28.3 us
  matrix products: 15.6 us -> 12.8 us
  local copies, waits for them, and re-layouts: 12.7 us -> 14.7 us
    all_gather x1 -> x0, waiting for transfers between devices: 53.8 us -> none  [body(): piece = lax.all_gather(hidden, 'tok', axis=0, tiled=True)]
    ppermute x0 -> x7, waiting for transfers between devices: none -> 28 us  [the longest x4 18.8 us: body(): lax.ppermute(going_up, 'tok', [(d, (d + 1) % ways) for d in range(ways)])]
    ppermute x0 -> x7, starting transfers between devices: none -> 24.9 us  [the longest x3 16.3 us: body(): lax.ppermute(going_down, 'tok', [(d, (d - 1) % ways) for d in range(ways)])]
    unnamed x2, blocking collectives: 18.7 us -> 28.3 us
    dynamic_update_slice x0 -> x8, local copies, waits for them, and re-layouts: none -> 2.3 us  [the longest x4 1.15 us: body(): lax.dynamic_update_slice_in_dim(piece, going_up, (here - far) % ways * st...]
    unnamed x22 -> x36, local copies, waits for them, and re-layouts: 7.34 us -> 6.75 us
  transfers between devices with their start and end apart: 8 -> 14, of which waited for: 8 -> 10; matrix products, arithmetic and copies ran while one was open for 2% -> 3% of each run, Pallas kernels for 0% -> 0%
where the time goes in v1:
time: 176 us; the launch traced here: 175 us
  waiting for transfers between devices  66.3 us (38%)
  starting transfers between devices  49 us (28%)
  blocking collectives  28.3 us (16%)
  local copies, waits for them, and re-layouts  14.7 us (8%)
  matrix products  12.8 us (7%)
  between operations  2.33 us (1%)
    all_to_all x7, waiting for transfers between devices, body(): lax.all_to_all(shaped, 'tok', split_axis=0, concat_axis=0, tiled=True)  38.3 us
    unnamed x2, blocking collectives  28.3 us
    all_to_all x7, starting transfers between devices, body(): lax.all_to_all(shaped, 'tok', split_axis=0, concat_axis=0, tiled=True)  24.1 us
    ppermute x4, waiting for transfers between devices, body(): lax.ppermute(going_up, 'tok', [(d, (d + 1) % ways) for d in range(ways)])  18.8 us
    ppermute x3, starting transfers between devices, body(): lax.ppermute(going_down, 'tok', [(d, (d - 1) % ways) for d in range(ways)])  16.3 us
    ppermute x3, waiting for transfers between devices, body(): lax.ppermute(going_down, 'tok', [(d, (d - 1) % ways) for d in range(ways)])  9.17 us
    dot_general x1, matrix products, body(): jnp.dot(piece, policy_head, preferred_element_type=jnp.float32)  8.64 us
    ppermute x4, starting transfers between devices, body(): lax.ppermute(going_up, 'tok', [(d, (d + 1) % ways) for d in range(ways)])  8.58 us
  transfers between devices with their start and end apart: 14, of which 10 were waited for; matrix products, arithmetic and copies ran while one was open for 3% of the time, Pallas kernels for 0%

profile of v1, /device:TPU:0, one launch (start us, length us, event | category | flops | bytes accessed | tf_op | source)
XLA Modules:
  0.0 175.1 jit_solution(15850145136698909493)
XLA Ops:
  0.7 3.0 %collective-permute-start = (bf16[24,9216]{1,0:T(8,128)(2,1)}, bf16[24,9216]{1,0:T(8,128)(2,1)}, u32[]{:S(2)}, u32[]{:S(2)}) collective-permute-start(bf16[24,9216]{1,0:T(8,128)(2,1)} %param.6), channel_id=1, source_target_pairs={{0,4},{4,8},{8,12},{12,16},{16,20},{20,24},{24,28},{28,0},{1,5},{5... | collective-permute-start | bytes 1327112 | tf_op jit(solution)/shard_map/ppermute | solution.py:90
  3.7 3.1 %collective-permute-start.1 = (bf16[24,9216]{1,0:T(8,128)(2,1)}, bf16[24,9216]{1,0:T(8,128)(2,1)}, u32[]{:S(2)}, u32[]{:S(2)}) collective-permute-start(bf16[24,9216]{1,0:T(8,128)(2,1)} %param.6), channel_id=1, source_target_pairs={{0,28},{4,0},{8,4},{12,8},{16,12},{20,16},{24,20},{28,24},{1,29},{... | collective-permute-start | bytes 1327112 | tf_op jit(solution)/shard_map/ppermute | solution.py:95
  6.8 0.4 broadcast_in_dim.7
  7.2 0.7 copy-done
  8.0 0.6 dynamic-slice.5
  9.3 0.2 dynamic-update-slice.5
  9.5 22.6 %all-reduce.5 = s32[192]{0:T(256)S(1)} all-reduce(s32[192]{0:T(256)S(1)} %dynamic-update-slice.5), channel_id=1, replica_groups=mesh['tok'=8,'vocab'=4] {'tok'}, use_global_device_ids=true, to_apply=%add.5 | all-reduce | flops 192 | bytes 1536
  32.2 0.7 collective-permute-start.2
  32.9 4.1 %collective-permute-start.3 = (bf16[24,9216]{1,0:T(8,128)(2,1)}, bf16[24,9216]{1,0:T(8,128)(2,1)S(1)}, u32[]{:S(2)}, u32[]{:S(2)}) collective-permute-start(bf16[24,9216]{1,0:T(8,128)(2,1)} %collective-permute-done.1), channel_id=1, source_target_pairs={{0,28},{4,0},{8,4},{12,8},{16,12},{20,16},{24,20},{28,24},{1,29},{... | collective-permute-start | bytes 1327112 | tf_op jit(solution)/shard_map/ppermute | solution.py:95
  37.0 1.0 constant_dynamic-update-slice_fusion.6
  38.0 1.1 constant_dynamic-update-slice_fusion.5
  39.1 11.2 %collective-permute-done.2 = bf16[24,9216]{1,0:T(8,128)(2,1)S(1)} collective-permute-done((bf16[24,9216]{1,0:T(8,128)(2,1)}, bf16[24,9216]{1,0:T(8,128)(2,1)S(1)}, u32[]{:S(2)}, u32[]{:S(2)}) %collective-permute-start.2) | collective-permute-done | bytes 442400 | tf_op jit(solution)/shard_map/ppermute | solution.py:90
  50.2 2.4 %collective-permute-start.4 = (bf16[24,9216]{1,0:T(8,128)(2,1)S(1)}, bf16[24,9216]{1,0:T(8,128)(2,1)S(1)}, u32[]{:S(2)}, u32[]{:S(2)}) collective-permute-start(bf16[24,9216]{1,0:T(8,128)(2,1)S(1)} %collective-permute-done.2), channel_id=1, source_target_pairs={{0,4},{4,8},{8,12},{12,16},{16,20},{20,24},{24,28},{28,0},{1,5},{5... | collective-permute-start | bytes 1327112 | tf_op jit(solution)/shard_map/ppermute | solution.py:90
  52.6 9.1 %collective-permute-start.5 = (bf16[24,9216]{1,0:T(8,128)(2,1)S(1)}, bf16[24,9216]{1,0:T(8,128)(2,1)S(1)}, u32[]{:S(2)}, u32[]{:S(2)}) collective-permute-start(bf16[24,9216]{1,0:T(8,128)(2,1)S(1)} %collective-permute-done.3), channel_id=1, source_target_pairs={{0,28},{4,0},{8,4},{12,8},{16,12},{20,16},{24,20},{28,24},{1,29},{... | collective-permute-start | bytes 1327112 | tf_op jit(solution)/shard_map/ppermute | solution.py:95
  61.8 7.6 %collective-permute-done.4 = bf16[24,9216]{1,0:T(8,128)(2,1)S(1)} collective-permute-done((bf16[24,9216]{1,0:T(8,128)(2,1)S(1)}, bf16[24,9216]{1,0:T(8,128)(2,1)S(1)}, u32[]{:S(2)}, u32[]{:S(2)}) %collective-permute-start.4) | collective-permute-done | bytes 442400 | tf_op jit(solution)/shard_map/ppermute | solution.py:90
  69.4 2.5 %collective-permute-start.6 = (bf16[24,9216]{1,0:T(8,128)(2,1)S(1)}, bf16[24,9216]{1,0:T(8,128)(2,1)S(1)}, u32[]{:S(2)}, u32[]{:S(2)}) collective-permute-start(bf16[24,9216]{1,0:T(8,128)(2,1)S(1)} %collective-permute-done.4), channel_id=1, source_target_pairs={{0,4},{4,8},{8,12},{12,16},{16,20},{20,24},{24,28},{28,0},{1,5},{5... | collective-permute-start | bytes 1327112 | tf_op jit(solution)/shard_map/ppermute | solution.py:90
  72.0 9.2 %collective-permute-done.5 = bf16[24,9216]{1,0:T(8,128)(2,1)S(1)} collective-permute-done((bf16[24,9216]{1,0:T(8,128)(2,1)S(1)}, bf16[24,9216]{1,0:T(8,128)(2,1)S(1)}, u32[]{:S(2)}, u32[]{:S(2)}) %collective-permute-start.5) | collective-permute-done | bytes 442400 | tf_op jit(solution)/shard_map/ppermute | solution.py:95
  81.3 8.6 %fusion.24 = (f32[192]{0:T(256)S(1)}, f32[192,1024]{1,0:T(8,128)S(1)}) fusion(bf16[192,9216]{1,0:T(8,128)(2,1)S(1)} %constant_dynamic-update-slice_fusion, bf16[9216,1024]{1,0:T(8,128)(2,1)} %param.7), kind=kOutput, calls=%fused_computation.52 | convolution fusion | flops 3624075008 | bytes 23200512 | tf_op jit(solution)/shard_map/dot_general | solution.py:101
  90.0 1.2 slice-done.2
  91.2 1.2 slice-done.3
  92.4 0.6 slice-done.4
  93.0 4.2 %fusion.25 = (f32[192]{0:T(256)S(1)}, f32[192,1024]{1,0:T(8,128)S(1)}) fusion(bf16[192,9216]{1,0:T(8,128)(2,1)S(1)} %constant_dynamic-update-slice_fusion, bf16[9216,1024]{1,0:T(8,128)(2,1)S(1)} %bitcast.83), kind=kOutput, calls=%fused_computation.53 | convolution fusion | flops 3624075008 | bytes 23200512 | tf_op jit(solution)/shard_map/dot_general | solution.py:102
  97.2 0.7 multiply_reduce_fusion
  97.9 0.7 all_to_all.60
  98.6 4.3 %all-to-all-start.3 = ((f32[8,1,24]{2,1,0:T(1,128)}), f32[8,1,24]{2,1,0:T(1,128)S(1)}, u32[]{:S(2)}, u32[]{:S(2)}) async-start(f32[8,1,24]{2,1,0:T(1,128)} %all_to_all.60), calls=%async_computation.3 | async-start | bytes 8192 | tf_op jit(solution)/shard_map/all_to_all | solution.py:114
  102.9 0.7 all_to_all.54
  103.6 5.8 %all-to-all-done.3 = f32[8,1,24]{2,1,0:T(1,128)S(1)} async-done(((f32[8,1,24]{2,1,0:T(1,128)}), f32[8,1,24]{2,1,0:T(1,128)S(1)}, u32[]{:S(2)}, u32[]{:S(2)}) %all-to-all-start.3) | async-done | bytes 800 | tf_op jit(solution)/shard_map/all_to_all | solution.py:114
  109.4 3.3 %all-to-all-start.1 = ((f32[8,1,24]{2,1,0:T(1,128)}), f32[8,1,24]{2,1,0:T(1,128)S(1)}, u32[]{:S(2)}, u32[]{:S(2)}) async-start(f32[8,1,24]{2,1,0:T(1,128)} %all_to_all.54), calls=%async_computation.1 | async-start | bytes 8192 | tf_op jit(solution)/shard_map/all_to_all | solution.py:114
  112.8 0.7 all_to_all.64
  113.4 5.8 %all-to-all-done.1 = f32[8,1,24]{2,1,0:T(1,128)S(1)} async-done(((f32[8,1,24]{2,1,0:T(1,128)}), f32[8,1,24]{2,1,0:T(1,128)S(1)}, u32[]{:S(2)}, u32[]{:S(2)}) %all-to-all-start.1) | async-done | bytes 800 | tf_op jit(solution)/shard_map/all_to_all | solution.py:114
  119.2 3.3 %all-to-all-start.4 = ((f32[8,1,24]{2,1,0:T(1,128)}), f32[8,1,24]{2,1,0:T(1,128)S(1)}, u32[]{:S(2)}, u32[]{:S(2)}) async-start(f32[8,1,24]{2,1,0:T(1,128)} %all_to_all.64), calls=%async_computation.4 | async-start | bytes 8192 | tf_op jit(solution)/shard_map/all_to_all | solution.py:114
  122.5 0.7 all_to_all.52
  123.2 5.7 %all-to-all-done.4 = f32[8,1,24]{2,1,0:T(1,128)S(1)} async-done(((f32[8,1,24]{2,1,0:T(1,128)}), f32[8,1,24]{2,1,0:T(1,128)S(1)}, u32[]{:S(2)}, u32[]{:S(2)}) %all-to-all-start.4) | async-done | bytes 800 | tf_op jit(solution)/shard_map/all_to_all | solution.py:114
  128.9 3.2 %all-to-all-start = ((f32[8,1,24]{2,1,0:T(1,128)}), f32[8,1,24]{2,1,0:T(1,128)S(1)}, u32[]{:S(2)}, u32[]{:S(2)}) async-start(f32[8,1,24]{2,1,0:T(1,128)} %all_to_all.52), calls=%async_computation | async-start | bytes 8192 | tf_op jit(solution)/shard_map/all_to_all | solution.py:114
  132.2 0.7 all_to_all.56
  132.8 5.7 %all-to-all-done = f32[8,1,24]{2,1,0:T(1,128)S(1)} async-done(((f32[8,1,24]{2,1,0:T(1,128)}), f32[8,1,24]{2,1,0:T(1,128)S(1)}, u32[]{:S(2)}, u32[]{:S(2)}) %all-to-all-start) | async-done | bytes 800 | tf_op jit(solution)/shard_map/all_to_all | solution.py:114
  138.6 3.3 %all-to-all-start.2 = ((f32[8,1,24]{2,1,0:T(1,128)}), f32[8,1,24]{2,1,0:T(1,128)S(1)}, u32[]{:S(2)}, u32[]{:S(2)}) async-start(f32[8,1,24]{2,1,0:T(1,128)} %all_to_all.56), calls=%async_computation.2 | async-start | bytes 8192 | tf_op jit(solution)/shard_map/all_to_all | solution.py:114
  141.9 0.6 dynamic-slice
  143.2 0.7 all_to_all.67
  143.9 0.7 all_to_all.69
  144.6 3.8 %all-to-all-done.2 = f32[8,1,24]{2,1,0:T(1,128)S(1)} async-done(((f32[8,1,24]{2,1,0:T(1,128)}), f32[8,1,24]{2,1,0:T(1,128)S(1)}, u32[]{:S(2)}, u32[]{:S(2)}) %all-to-all-start.2) | async-done | bytes 800 | tf_op jit(solution)/shard_map/all_to_all | solution.py:114
  148.4 3.2 %all-to-all-start.5 = ((f32[8,1,24]{2,1,0:T(1,128)}), f32[8,1,24]{2,1,0:T(1,128)S(1)}, u32[]{:S(2)}, u32[]{:S(2)}) async-start(f32[8,1,24]{2,1,0:T(1,128)} %all_to_all.67), calls=%async_computation.5 | async-start | bytes 8192 | tf_op jit(solution)/shard_map/all_to_all | solution.py:114
  151.7 6.4 %all-to-all-done.5 = f32[8,1,24]{2,1,0:T(1,128)S(1)} async-done(((f32[8,1,24]{2,1,0:T(1,128)}), f32[8,1,24]{2,1,0:T(1,128)S(1)}, u32[]{:S(2)}, u32[]{:S(2)}) %all-to-all-start.5) | async-done | bytes 800 | tf_op jit(solution)/shard_map/all_to_all | solution.py:114
  158.0 3.3 %all-to-all-start.6 = ((f32[8,1,24]{2,1,0:T(1,128)}), f32[8,1,24]{2,1,0:T(1,128)S(1)}, u32[]{:S(2)}, u32[]{:S(2)}) async-start(f32[8,1,24]{2,1,0:T(1,128)} %all_to_all.69), calls=%async_computation.6 | async-start | bytes 8192 | tf_op jit(solution)/shard_map/all_to_all | solution.py:114
  162.7 5.1 %all-to-all-done.6 = f32[8,1,24]{2,1,0:T(1,128)S(1)} async-done(((f32[8,1,24]{2,1,0:T(1,128)}), f32[8,1,24]{2,1,0:T(1,128)S(1)}, u32[]{:S(2)}, u32[]{:S(2)}) %all-to-all-start.6) | async-done | bytes 800 | tf_op jit(solution)/shard_map/all_to_all | solution.py:114
  168.0 5.6 %all-reduce.8 = (f32[96]{0:T(128)S(1)}, f32[96]{0:T(128)S(1)}, f32[96]{0:T(128)S(1)}, f32[96]{0:T(128)S(1)}, f32[96]{0:T(128)S(1)}, /*index=5*/f32[96]{0:T(128)S(1)}, f32[96]{0:T(128)S(1)}) all-reduce(f32[96]{0:T(128)S(1)} %dynamic-update-slice, f32[96]{0:T(128)S(1)} %dynamic-update-slice.1, ...), channel_id=2, replica_groups=mesh['tok'=8,'vocab'=4] {'vocab'}, use_global_device_ids=true, to_apply=%add | all-reduce | flops 672 | bytes 5376
  174.2 0.3 while.27
  174.5 0.5 subtract_add_fusion
  (66 shorter events, 2.8 us)
Async XLA Ops:
  0.6 7.4 %copy-start.3 = (u32[32]{0:T(128)S(1)}, u32[32]{0:T(128)}, u32[]{:S(2)}) copy-start(u32[32]{0:T(128)} %constant.137) | copy-start | bytes 388
  0.6 8.6 %copy-start.1 = (s32[24]{0:T(128)S(1)}, s32[24]{0:T(128)}, u32[]{:S(2)}) copy-start(s32[24]{0:T(128)} %param.9) | copy-start | bytes 292
  0.7 31.5 %collective-permute-start = (bf16[24,9216]{1,0:T(8,128)(2,1)}, bf16[24,9216]{1,0:T(8,128)(2,1)}, u32[]{:S(2)}, u32[]{:S(2)}) collective-permute-start(bf16[24,9216]{1,0:T(8,128)(2,1)} %param.6), channel_id=1, source_target_pairs={{0,4},{4,8},{8,12},{12,16},{16,20},{20,24},{24,28},{28,0},{1,5},{5... | collective-permute-start | bytes 1327112 | tf_op jit(solution)/shard_map/ppermute | solution.py:90
  3.7 29.2 %collective-permute-start.1 = (bf16[24,9216]{1,0:T(8,128)(2,1)}, bf16[24,9216]{1,0:T(8,128)(2,1)}, u32[]{:S(2)}, u32[]{:S(2)}) collective-permute-start(bf16[24,9216]{1,0:T(8,128)(2,1)} %param.6), channel_id=1, source_target_pairs={{0,28},{4,0},{8,4},{12,8},{16,12},{20,16},{24,20},{28,24},{1,29},{... | collective-permute-start | bytes 1327112 | tf_op jit(solution)/shard_map/ppermute | solution.py:95
  6.8 1.0 copy-start
  32.2 18.0 %collective-permute-start.2 = (bf16[24,9216]{1,0:T(8,128)(2,1)}, bf16[24,9216]{1,0:T(8,128)(2,1)S(1)}, u32[]{:S(2)}, u32[]{:S(2)}) collective-permute-start(bf16[24,9216]{1,0:T(8,128)(2,1)} %collective-permute-done), channel_id=1, source_target_pairs={{0,4},{4,8},{8,12},{12,16},{16,20},{20,24},{24,28},{28,0},{1,5},{5... | collective-permute-start | bytes 1327112 | tf_op jit(solution)/shard_map/ppermute | solution.py:90
  32.9 19.7 %collective-permute-start.3 = (bf16[24,9216]{1,0:T(8,128)(2,1)}, bf16[24,9216]{1,0:T(8,128)(2,1)S(1)}, u32[]{:S(2)}, u32[]{:S(2)}) collective-permute-start(bf16[24,9216]{1,0:T(8,128)(2,1)} %collective-permute-done.1), channel_id=1, source_target_pairs={{0,28},{4,0},{8,4},{12,8},{16,12},{20,16},{24,20},{28,24},{1,29},{... | collective-permute-start | bytes 1327112 | tf_op jit(solution)/shard_map/ppermute | solution.py:95
  50.2 19.2 %collective-permute-start.4 = (bf16[24,9216]{1,0:T(8,128)(2,1)S(1)}, bf16[24,9216]{1,0:T(8,128)(2,1)S(1)}, u32[]{:S(2)}, u32[]{:S(2)}) collective-permute-start(bf16[24,9216]{1,0:T(8,128)(2,1)S(1)} %collective-permute-done.2), channel_id=1, source_target_pairs={{0,4},{4,8},{8,12},{12,16},{16,20},{20,24},{24,28},{28,0},{1,5},{5... | collective-permute-start | bytes 1327112 | tf_op jit(solution)/shard_map/ppermute | solution.py:90
  52.6 28.5 %collective-permute-start.5 = (bf16[24,9216]{1,0:T(8,128)(2,1)S(1)}, bf16[24,9216]{1,0:T(8,128)(2,1)S(1)}, u32[]{:S(2)}, u32[]{:S(2)}) collective-permute-start(bf16[24,9216]{1,0:T(8,128)(2,1)S(1)} %collective-permute-done.3), channel_id=1, source_target_pairs={{0,28},{4,0},{8,4},{12,8},{16,12},{20,16},{24,20},{28,24},{1,29},{... | collective-permute-start | bytes 1327112 | tf_op jit(solution)/shard_map/ppermute | solution.py:95
  69.4 11.7 %collective-permute-start.6 = (bf16[24,9216]{1,0:T(8,128)(2,1)S(1)}, bf16[24,9216]{1,0:T(8,128)(2,1)S(1)}, u32[]{:S(2)}, u32[]{:S(2)}) collective-permute-start(bf16[24,9216]{1,0:T(8,128)(2,1)S(1)} %collective-permute-done.4), channel_id=1, source_target_pairs={{0,4},{4,8},{8,12},{12,16},{16,20},{20,24},{24,28},{28,0},{1,5},{5... | collective-permute-start | bytes 1327112 | tf_op jit(solution)/shard_map/ppermute | solution.py:90
  81.2 8.7 %slice-start = ((s8[18874368]{0:T(1024)(128)(4,1)}), s8[4194304]{0:T(1024)(128)(4,1)S(1)}, s32[]{:S(2)}) async-start(s8[18874368]{0:T(1024)(128)(4,1)} %bitcast.82), calls=%async_computation.7 | async-start | bytes 8388608
  81.2 8.8 %slice-start.1 = ((s8[18874368]{0:T(1024)(128)(4,1)}), s8[4194304]{0:T(1024)(128)(4,1)S(1)}, s32[]{:S(2)}) async-start(s8[18874368]{0:T(1024)(128)(4,1)} %bitcast.82), calls=%async_computation.8 | async-start | bytes 8388608
  81.2 10.0 %slice-start.2 = ((s8[18874368]{0:T(1024)(128)(4,1)}), s8[4194304]{0:T(1024)(128)(4,1)S(1)}, s32[]{:S(2)}) async-start(s8[18874368]{0:T(1024)(128)(4,1)} %bitcast.82), calls=%async_computation.9 | async-start | bytes 8388608
  81.3 11.2 %slice-start.3 = ((s8[18874368]{0:T(1024)(128)(4,1)}), s8[4194304]{0:T(1024)(128)(4,1)S(1)}, s32[]{:S(2)}) async-start(s8[18874368]{0:T(1024)(128)(4,1)} %bitcast.82), calls=%async_computation.10 | async-start | bytes 8388608
  81.3 11.8 %slice-start.4 = ((s8[18874368]{0:T(1024)(128)(4,1)}), s8[2097152]{0:T(1024)(128)(4,1)S(1)}, s32[]{:S(2)}) async-start(s8[18874368]{0:T(1024)(128)(4,1)} %bitcast.82), calls=%async_computation.11 | async-start | bytes 4194304
  93.0 48.9 %copy-start.2 = (u32[32]{0:T(128)S(1)}, u32[32]{0:T(128)}, u32[]{:S(2)}) copy-start(u32[32]{0:T(128)} %constant.112) | copy-start | bytes 388
  98.6 10.8 %all-to-all-start.3 = ((f32[8,1,24]{2,1,0:T(1,128)}), f32[8,1,24]{2,1,0:T(1,128)S(1)}, u32[]{:S(2)}, u32[]{:S(2)}) async-start(f32[8,1,24]{2,1,0:T(1,128)} %all_to_all.60), calls=%async_computation.3 | async-start | bytes 8192 | tf_op jit(solution)/shard_map/all_to_all | solution.py:114
  109.4 9.8 %all-to-all-start.1 = ((f32[8,1,24]{2,1,0:T(1,128)}), f32[8,1,24]{2,1,0:T(1,128)S(1)}, u32[]{:S(2)}, u32[]{:S(2)}) async-start(f32[8,1,24]{2,1,0:T(1,128)} %all_to_all.54), calls=%async_computation.1 | async-start | bytes 8192 | tf_op jit(solution)/shard_map/all_to_all | solution.py:114
  119.2 9.7 %all-to-all-start.4 = ((f32[8,1,24]{2,1,0:T(1,128)}), f32[8,1,24]{2,1,0:T(1,128)S(1)}, u32[]{:S(2)}, u32[]{:S(2)}) async-start(f32[8,1,24]{2,1,0:T(1,128)} %all_to_all.64), calls=%async_computation.4 | async-start | bytes 8192 | tf_op jit(solution)/shard_map/all_to_all | solution.py:114
  128.9 9.7 %all-to-all-start = ((f32[8,1,24]{2,1,0:T(1,128)}), f32[8,1,24]{2,1,0:T(1,128)S(1)}, u32[]{:S(2)}, u32[]{:S(2)}) async-start(f32[8,1,24]{2,1,0:T(1,128)} %all_to_all.52), calls=%async_computation | async-start | bytes 8192 | tf_op jit(solution)/shard_map/all_to_all | solution.py:114
  138.6 9.8 %all-to-all-start.2 = ((f32[8,1,24]{2,1,0:T(1,128)}), f32[8,1,24]{2,1,0:T(1,128)S(1)}, u32[]{:S(2)}, u32[]{:S(2)}) async-start(f32[8,1,24]{2,1,0:T(1,128)} %all_to_all.56), calls=%async_computation.2 | async-start | bytes 8192 | tf_op jit(solution)/shard_map/all_to_all | solution.py:114
  148.4 9.7 %all-to-all-start.5 = ((f32[8,1,24]{2,1,0:T(1,128)}), f32[8,1,24]{2,1,0:T(1,128)S(1)}, u32[]{:S(2)}, u32[]{:S(2)}) async-start(f32[8,1,24]{2,1,0:T(1,128)} %all_to_all.67), calls=%async_computation.5 | async-start | bytes 8192 | tf_op jit(solution)/shard_map/all_to_all | solution.py:114
  158.0 9.7 %all-to-all-start.6 = ((f32[8,1,24]{2,1,0:T(1,128)}), f32[8,1,24]{2,1,0:T(1,128)S(1)}, u32[]{:S(2)}, u32[]{:S(2)}) async-start(f32[8,1,24]{2,1,0:T(1,128)} %all_to_all.69), calls=%async_computation.6 | async-start | bytes 8192 | tf_op jit(solution)/shard_map/all_to_all | solution.py:114
